TPU v7x, 32 devices: a whole 2x2x4 slice. The times are simulated.
32 devices in a mesh: head: 8 (over z, core), kv: 4 (over y, x).
Axes of the slice: x: 2, y: 2, z: 4, core: 2. Of those that a mesh axis runs over, the one named last changes fastest.
Arguments:
- queries: bfloat16 [2048, 8192], P(('kv', 'head')), may hold values from -6 to 6
- key_rows: bfloat16 [2048, 1024], P(('kv', 'head')), may hold values from -6 to 6
- value_matrix: bfloat16 [2048, 1024], P(('kv', 'head')), may hold values from -6 to 6
- doc_ids: int32 [2048], P(('kv', 'head')), may hold values from 0 to 5, as said below
Outputs:
- attended: bfloat16 [2048, 8192], P(('kv', 'head'))
Inputs may be any that keep to these rules, and one draw needn't show every extreme that they name: doc_ids starts at 0, never falls, and rises by one at the first token of each of the 6 documents; every document starts at an even position and has 2 tokens or more.
All inputs are finite; a program needn't handle non-finite values.
Results may differ from a plain program's by a relative error of at most 0.015.
Values may be sent and summed in bfloat16 or wider, within the bound.
A program may use at most 64 MiB of HBM per device.

v0:
```python
import math
import jax
import jax.numpy as jnp
from jax import lax
from jax.sharding import PartitionSpec as P

QUERY_HEADS = 64
KEY_VALUE_HEADS = 8
HEAD_SIZE = 128
NEG_FILL = -1e30


def repeat_heads(input_matrix, head_repeats):
    row_number = input_matrix.shape[0]
    heads_apart = input_matrix.reshape(row_number, KEY_VALUE_HEADS, 1, HEAD_SIZE)
    expanded_heads = jnp.broadcast_to(
        heads_apart, (row_number, KEY_VALUE_HEADS, head_repeats, HEAD_SIZE)
    )
    return expanded_heads.reshape(row_number, KEY_VALUE_HEADS * head_repeats * HEAD_SIZE)


def block_terms(query_group, query_pos, query_doc, key_block, value_block, key_pos, key_doc):
    key_count = key_block.shape[0]
    key_value_slot = query_group.shape[1]
    key_heads = key_block.reshape(key_count, key_value_slot, HEAD_SIZE)
    value_heads = value_block.reshape(key_count, key_value_slot, HEAD_SIZE)
    scores = jnp.einsum(
        "rkgd,ckd->kgrc", query_group, key_heads, preferred_element_type=jnp.float32
    ) * HEAD_SIZE ** (-0.5)
    allowed = (key_pos[None, :] <= query_pos[:, None]) & (key_doc[None, :] == query_doc[:, None])
    masked = jnp.where(allowed, scores, NEG_FILL)
    row_peak = jnp.max(masked, axis=-1)
    weights = jnp.where(allowed, jnp.exp(masked - row_peak[..., None]), 0.0)
    row_total = jnp.sum(weights, axis=-1)
    weighted = jnp.einsum(
        "kgrc,ckd->kgrd",
        weights.astype(jnp.bfloat16),
        value_heads,
        preferred_element_type=jnp.float32,
    )
    return (row_peak, row_total, weighted)


def attend_block(query_group, query_pos, query_doc, key_block, value_block, key_pos, key_doc):
    return block_terms(query_group, query_pos, query_doc, key_block, value_block, key_pos, key_doc)


def combine_terms(first_terms, second_terms):
    joint_peak = jnp.maximum(first_terms[0], second_terms[0])
    left_factor = jnp.exp(first_terms[0] - joint_peak)
    right_factor = jnp.exp(second_terms[0] - joint_peak)
    joint_total = first_terms[1] * left_factor + second_terms[1] * right_factor
    joint_weighted = (
        first_terms[2] * left_factor[..., None] + second_terms[2] * right_factor[..., None]
    )
    return (joint_peak, joint_total, joint_weighted)


def local(queries, key_rows, value_matrix, doc_ids):
    head_number = lax.axis_size("head")
    head_repeats = max(1, head_number // KEY_VALUE_HEADS)
    key_send = repeat_heads(key_rows, head_repeats)
    value_send = repeat_heads(value_matrix, head_repeats)
    query_block, key_block, value_block = (
        lax.all_to_all(queries, "head", split_axis=1, concat_axis=0, tiled=True),
        lax.all_to_all(key_send, "head", split_axis=1, concat_axis=0, tiled=True),
        lax.all_to_all(value_send, "head", split_axis=1, concat_axis=0, tiled=True),
    )
    block_len = query_block.shape[0]
    doc_global = lax.all_gather(doc_ids, ("kv", "head"), axis=0, tiled=True)
    query_width = query_block.shape[1]
    present_heads = query_width // HEAD_SIZE
    key_value_slot = max(1, present_heads // (QUERY_HEADS // KEY_VALUE_HEADS))
    group_here = present_heads // key_value_slot
    own_first = lax.axis_index("kv") * block_len
    own_pos = own_first + jnp.arange(block_len, dtype=jnp.int32)
    own_doc = jnp.take(doc_global, own_pos)
    query_group = query_block.reshape(block_len, key_value_slot, group_here, HEAD_SIZE)
    term_shape = (key_value_slot, group_here, block_len)
    initial = (
        jnp.full(term_shape, NEG_FILL, jnp.float32),
        jnp.zeros(term_shape, jnp.float32),
        jnp.zeros(term_shape + (HEAD_SIZE,), jnp.float32),
    )
    key_piece = lax.all_gather(key_block, "kv", axis=0, tiled=True)
    value_piece = lax.all_gather(value_block, "kv", axis=0, tiled=True)
    piece_rows = key_piece.shape[0]
    step_rows = math.gcd(piece_rows, 1024)

    def one_step(step_index, inner):
        local_first = step_index * step_rows
        keys_now = lax.dynamic_slice_in_dim(key_piece, local_first, step_rows, 0)
        values_now = lax.dynamic_slice_in_dim(value_piece, local_first, step_rows, 0)
        key_pos = local_first + jnp.arange(step_rows, dtype=jnp.int32)
        key_doc = jnp.take(doc_global, key_pos)
        return combine_terms(
            inner,
            attend_block(query_group, own_pos, own_doc, keys_now, values_now, key_pos, key_doc),
        )

    folded = lax.fori_loop(0, piece_rows // step_rows, one_step, initial)
    result = (
        (folded[2] / folded[1][..., None]).transpose(2, 0, 1, 3).reshape(block_len, query_width)
    )
    result = result.astype(jnp.bfloat16)
    return lax.all_to_all(result, "head", split_axis=0, concat_axis=1, tiled=True)


def solution(mesh):
    return jax.shard_map(
        local,
        mesh=mesh,
        in_specs=(
            P(("kv", "head"), None),
            P(("kv", "head"), None),
            P(("kv", "head"), None),
            P(("kv", "head")),
        ),
        out_specs=P(("kv", "head"), None),
        check_vma=False,
    )
```

profile of v0, /device:TPU:0, one launch (start us, length us, event | category | flops | bytes accessed | tf_op | source)
XLA Modules:
  0.0 176.7 jit_solution(10033229204570758715)
XLA Ops:
  0.0 0.0 copy-start
  0.0 0.9 copy-done
  0.9 0.7 copy_bitcast_fusion.2
  1.6 6.4 %all-to-all-start = ((bf16[64,8,128]{2,0,1:T(8,128)(2,1)}), bf16[64,8,128]{2,0,1:T(8,128)(2,1)S(1)}, u32[]{:S(2)}, u32[]{:S(2)}) async-start(bf16[64,8,128]{2,0,1:T(8,128)(2,1)} %copy_bitcast_fusion.2), calls=%async_computation | async-start | bytes 262144 | tf_op jit(solution)/shard_map/all_to_all | solution.py:66
  7.9 1.6 copy_bitcast_fusion.1
  9.5 5.2 %all-to-all-done = bf16[64,8,128]{2,0,1:T(8,128)(2,1)S(1)} async-done(((bf16[64,8,128]{2,0,1:T(8,128)(2,1)}), bf16[64,8,128]{2,0,1:T(8,128)(2,1)S(1)}, u32[]{:S(2)}, u32[]{:S(2)}) %all-to-all-start) | async-done | bytes 131104 | tf_op jit(solution)/shard_map/all_to_all | solution.py:66
  14.7 3.4 %all-to-all-start.2 = ((bf16[64,8,128]{2,0,1:T(8,128)(2,1)}), bf16[64,8,128]{2,0,1:T(8,128)(2,1)S(1)}, u32[]{:S(2)}, u32[]{:S(2)}) async-start(bf16[64,8,128]{2,0,1:T(8,128)(2,1)} %copy_bitcast_fusion.1), calls=%async_computation.2 | async-start | bytes 262144 | tf_op jit(solution)/shard_map/all_to_all | solution.py:67
  18.1 2.3 %copy.30 = bf16[8,8,8,1024]{3,2,0,1:T(8,128)(2,1)} copy(bf16[8,8,8,1024]{3,2,1,0:T(8,128)(2,1)} %bitcast.121) | data formatting | bytes 2097152 | tf_op jit(solution)/shard_map/all_to_all | solution.py:65
  20.4 4.4 %all-to-all-done.2 = bf16[64,8,128]{2,0,1:T(8,128)(2,1)S(1)} async-done(((bf16[64,8,128]{2,0,1:T(8,128)(2,1)}), bf16[64,8,128]{2,0,1:T(8,128)(2,1)S(1)}, u32[]{:S(2)}, u32[]{:S(2)}) %all-to-all-start.2) | async-done | bytes 131104 | tf_op jit(solution)/shard_map/all_to_all | solution.py:67
  24.8 3.6 %all-to-all-start.1 = ((bf16[64,8,1024]{2,0,1:T(8,128)(2,1)}), bf16[64,8,1024]{2,0,1:T(8,128)(2,1)S(1)}, u32[]{:S(2)}, u32[]{:S(2)}) async-start(bf16[64,8,1024]{2,0,1:T(8,128)(2,1)} %bitcast.93), calls=%async_computation.1 | async-start | bytes 2097152 | tf_op jit(solution)/shard_map/all_to_all | solution.py:65
  28.4 1.3 dynamic-slice
  30.4 0.9 dynamic-update-slice
  31.2 43.9 %all-reduce = s32[2048]{0:T(1024)S(1)} all-reduce(s32[2048]{0:T(1024)S(1)} %dynamic-update-slice), channel_id=1, replica_groups=mesh['head'=8,'kv'=4] {'kv','head'}, use_global_device_ids=true, to_apply=%add | all-reduce | flops 2048 | bytes 16384
  75.2 3.1 %gather_fusion.1 = s32[512]{0:T(512)S(1)} fusion(s32[2048]{0:T(1024)S(1)} %all-reduce, s32[1024]{0:T(1024)S(1)} %pad_clamp_fusion), kind=kCustom, calls=%fused_computation.1 | custom fusion | bytes 6144 | tf_op jit(solution)/shard_map/jit(_take)/gather | solution.py:77
  78.3 11.6 %all_gather.11 = bf16[2048,128]{1,0:T(8,128)(2,1)S(1)} all-gather(bf16[512,128]{1,0:T(8,128)(2,1)S(1)} %bitcast.124), channel_id=1, replica_groups=mesh['head'=8,'kv'=4] {'kv'}, dimensions={0}, use_global_device_ids=true | all-gather | bytes 655360 | tf_op jit(solution)/shard_map/all_gather | solution.py:86
  89.9 9.0 %all_gather.10 = bf16[2048,128]{1,0:T(8,128)(2,1)S(1)} all-gather(bf16[512,128]{1,0:T(8,128)(2,1)S(1)} %bitcast.123), channel_id=1, replica_groups=mesh['head'=8,'kv'=4] {'kv'}, dimensions={0}, use_global_device_ids=true | all-gather | bytes 655360 | tf_op jit(solution)/shard_map/all_gather | solution.py:85
  98.9 0.0 all-to-all-done.1
  98.9 0.3 copy.26
  99.2 0.1 copy.18
  99.3 43.2 %while.18 = (s32[]{:T(128)}, f32[1,8,512]{2,1,0:T(8,128)S(1)}, f32[1,8,512]{2,1,0:T(8,128)S(1)}, f32[1,8,512,128]{3,2,1,0:T(8,128)}, s32[2048]{0:T(1024)S(1)}, /...) while((s32[]{:T(128)}, f32[1,8,512]{2,1,0:T(8,128)S(1)}, ...), condition=%wide.region_3.4_spmd.clone, body=%wide.region_0.3_spmd.clone.sunk | while | flops 2205726208 | bytes 75335952 | solution.py:101
  99.4 6.2 %gather_fusion = s32[1024]{0:T(1024)S(1)} fusion(s32[2048]{0:T(1024)S(1)} %get-tuple-element.370, s32[1024]{0:T(1024)S(1)} %broadcast_clamp_fusion.2), kind=kCustom, calls=%fused_computation.clone.clone.1 | custom fusion | bytes 12288 | tf_op jit(solution)/shard_map/while/body/eval_jaxpr/jit(_take)/gather | solution.py:95
  105.6 0.8 compare_and_fusion.2
  106.4 2.9 %fusion.41 = (f32[8,512]{1,0:T(8,128)S(1)}, f32[1024,512,8]{1,0,2:T(8,128)S(1)}) fusion(pred[512,1024]{0,1:T(8,128)(4,1)S(1)} %compare_and_fusion.2, bf16[512,1,8,128]{3,0,2,1:T(8,128)(2,1)S(1)} %get-tuple-element.373, bf16[2048,128]{1,0:T(8,128)(2,1)S(1)} %get-tuple-element.372, s32[]{:T(128)S(6)} %select_n.145), kind=kOutput, calls=%fused_computation.5.clone.1 | convolution fusion | flops 1086320640 | bytes 18628612 | tf_op jit(solution)/shard_map/while/body/eval_jaxpr/rkgd,ckd->kgrc/dot_general | solution.py:27
  109.3 0.0 copy-start.1
  109.3 4.0 %fusion.43 = f32[8,512]{1,0:T(8,128)S(1)} fusion(f32[1024,512,8]{1,0,2:T(8,128)S(1)} %get-tuple-element.334, f32[8,512]{1,0:T(8,128)S(1)} %get-tuple-element.332, pred[512,1024]{0,1:T(8,128)(4,1)S(1)} %compare_and_fusion.2), kind=kLoop, calls=%fused_computation.7.clone.1 | loop fusion | flops 20967424 | bytes 17334272 | tf_op jit(solution)/shard_map/while/body/eval_jaxpr/reduce_sum | solution.py:34
  113.4 0.0 copy-done.1
  113.4 6.1 %bitcast_add_fusion.2 = f32[1,8,512,128]{3,2,1,0:T(8,128)S(1)} fusion(f32[1,8,512,128]{3,2,1,0:T(8,128)S(1)} %copy-done.1, f32[1024,512,8]{1,0,2:T(8,128)S(1)} %get-tuple-element.334, f32[8,512]{1,0:T(8,128)S(1)} %get-tuple-element.332, pred[512,1024]{0,1:T(8,128)(4,1)S(1)} %compare_and_fusion.2, f32[8,512]{1,0:T(8,128)S(1)} %get-tuple-element.336, ...), kind=kOutput, calls=%fused_computation.11.clone.1 | convolution fusion | flops 1096810496 | bytes 21807108 | tf_op jit(solution)/shard_map/while/body/eval_jaxpr/kgrc,ckd->kgrd/dot_general | solution.py:35
  119.6 0.0 copy-start.2
  119.6 1.3 copy-done.2
  120.9 6.2 %gather_fusion = s32[1024]{0:T(1024)S(1)} fusion(s32[2048]{0:T(1024)S(1)} %get-tuple-element.370, s32[1024]{0:T(1024)S(1)} %broadcast_clamp_fusion.2), kind=kCustom, calls=%fused_computation.clone.clone.1 | custom fusion | bytes 12288 | tf_op jit(solution)/shard_map/while/body/eval_jaxpr/jit(_take)/gather | solution.py:95
  127.1 0.8 compare_and_fusion.2
  128.0 2.9 %fusion.41 = (f32[8,512]{1,0:T(8,128)S(1)}, f32[1024,512,8]{1,0,2:T(8,128)S(1)}) fusion(pred[512,1024]{0,1:T(8,128)(4,1)S(1)} %compare_and_fusion.2, bf16[512,1,8,128]{3,0,2,1:T(8,128)(2,1)S(1)} %get-tuple-element.373, bf16[2048,128]{1,0:T(8,128)(2,1)S(1)} %get-tuple-element.372, s32[]{:T(128)S(6)} %select_n.145), kind=kOutput, calls=%fused_computation.5.clone.1 | convolution fusion | flops 1086320640 | bytes 18628612 | tf_op jit(solution)/shard_map/while/body/eval_jaxpr/rkgd,ckd->kgrc/dot_general | solution.py:27
  130.9 0.0 copy-start.1
  130.9 4.0 %fusion.43 = f32[8,512]{1,0:T(8,128)S(1)} fusion(f32[1024,512,8]{1,0,2:T(8,128)S(1)} %get-tuple-element.334, f32[8,512]{1,0:T(8,128)S(1)} %get-tuple-element.332, pred[512,1024]{0,1:T(8,128)(4,1)S(1)} %compare_and_fusion.2), kind=kLoop, calls=%fused_computation.7.clone.1 | loop fusion | flops 20967424 | bytes 17334272 | tf_op jit(solution)/shard_map/while/body/eval_jaxpr/reduce_sum | solution.py:34
  135.0 0.0 copy-done.1
  135.0 6.1 %bitcast_add_fusion.2 = f32[1,8,512,128]{3,2,1,0:T(8,128)S(1)} fusion(f32[1,8,512,128]{3,2,1,0:T(8,128)S(1)} %copy-done.1, f32[1024,512,8]{1,0,2:T(8,128)S(1)} %get-tuple-element.334, f32[8,512]{1,0:T(8,128)S(1)} %get-tuple-element.332, pred[512,1024]{0,1:T(8,128)(4,1)S(1)} %compare_and_fusion.2, f32[8,512]{1,0:T(8,128)S(1)} %get-tuple-element.336, ...), kind=kOutput, calls=%fused_computation.11.clone.1 | convolution fusion | flops 1096810496 | bytes 21807108 | tf_op jit(solution)/shard_map/while/body/eval_jaxpr/kgrc,ckd->kgrd/dot_general | solution.py:35
  141.1 0.0 copy-start.2
  141.2 1.3 copy-done.2
  142.5 2.0 %fusion.26 = bf16[512,1,8,128]{3,0,2,1:T(8,128)(2,1)S(1)} fusion(f32[1,8,512,128]{3,2,1,0:T(8,128)} %get-tuple-element.175, f32[8,512]{1,0:T(8,128)S(1)} %bitcast.122), kind=kLoop, calls=%fused_computation.42 | loop fusion | flops 1048576 | bytes 3162112 | tf_op jit(solution)/shard_map/convert_element_type | solution.py:105
  144.4 0.7 copy.19
  145.1 0.5 convert_element_type.19
  145.6 30.0 %all_to_all.70 = bf16[8,64,1024]{2,1,0:T(8,128)(2,1)S(1)} all-to-all(bf16[8,64,1024]{2,1,0:T(8,128)(2,1)S(1)} %convert_element_type.19), channel_id=1, replica_groups=mesh['head'=8,'kv'=4] {'head'}, dimensions={0} | all-to-all | bytes 2097152 | tf_op jit(solution)/shard_map/all_to_all | solution.py:106
  175.6 1.1 copy.25
  (21 shorter events, 0.2 us)
Async XLA Ops:
  0.0 0.9 copy-start
  1.6 13.1 %all-to-all-start = ((bf16[64,8,128]{2,0,1:T(8,128)(2,1)}), bf16[64,8,128]{2,0,1:T(8,128)(2,1)S(1)}, u32[]{:S(2)}, u32[]{:S(2)}) async-start(bf16[64,8,128]{2,0,1:T(8,128)(2,1)} %copy_bitcast_fusion.2), calls=%async_computation | async-start | bytes 262144 | tf_op jit(solution)/shard_map/all_to_all | solution.py:66
  14.7 10.1 %all-to-all-start.2 = ((bf16[64,8,128]{2,0,1:T(8,128)(2,1)}), bf16[64,8,128]{2,0,1:T(8,128)(2,1)S(1)}, u32[]{:S(2)}, u32[]{:S(2)}) async-start(bf16[64,8,128]{2,0,1:T(8,128)(2,1)} %copy_bitcast_fusion.1), calls=%async_computation.2 | async-start | bytes 262144 | tf_op jit(solution)/shard_map/all_to_all | solution.py:67
  24.8 74.1 %all-to-all-start.1 = ((bf16[64,8,1024]{2,0,1:T(8,128)(2,1)}), bf16[64,8,1024]{2,0,1:T(8,128)(2,1)S(1)}, u32[]{:S(2)}, u32[]{:S(2)}) async-start(bf16[64,8,1024]{2,0,1:T(8,128)(2,1)} %bitcast.93), calls=%async_computation.1 | async-start | bytes 2097152 | tf_op jit(solution)/shard_map/all_to_all | solution.py:65
  109.3 4.1 %copy-start.1 = (f32[1,8,512,128]{3,2,1,0:T(8,128)S(1)}, f32[1,8,512,128]{3,2,1,0:T(8,128)}, u32[]{:S(2)}) copy-start(f32[1,8,512,128]{3,2,1,0:T(8,128)} %get-tuple-element.355) | copy-start | bytes 6291460 | tf_op jit(solution)/shard_map/while
  119.6 1.3 copy-start.2
  130.9 4.1 %copy-start.1 = (f32[1,8,512,128]{3,2,1,0:T(8,128)S(1)}, f32[1,8,512,128]{3,2,1,0:T(8,128)}, u32[]{:S(2)}) copy-start(f32[1,8,512,128]{3,2,1,0:T(8,128)} %get-tuple-element.355) | copy-start | bytes 6291460 | tf_op jit(solution)/shard_map/while
  141.1 1.3 copy-start.2
where the time goes:
time: 177 us
  blocking collectives  94.4 us (53%)
  local copies, waits for them, and re-layouts  28.4 us (16%)
  matrix products  18.1 us (10%)
  starting transfers between devices  13.3 us (8%)
  other arithmetic  11.8 us (7%)
  waiting for transfers between devices  9.58 us (5%)
    unnamed x1, blocking collectives  43.9 us
    all_to_all x1, blocking collectives, local(): lax.all_to_all(result, 'head', split_axis=0, concat_axis=1, tiled=True)  30 us
    gather x2, local copies, waits for them, and re-layouts, one_step(): key_doc = jnp.take(doc_global, key_pos)  12.3 us
    dot_general x2, matrix products, block_terms(): jnp.einsum('kgrc,ckd->kgrd', weights.astype(jnp.bfloat16), value_heads, p...  12.3 us
    all_gather x1, blocking collectives, local(): value_piece = lax.all_gather(value_block, 'kv', axis=0, tiled=True)  11.6 us
    all_gather x1, blocking collectives, local(): key_piece = lax.all_gather(key_block, 'kv', axis=0, tiled=True)  9 us
    reduce_sum x2, other arithmetic, block_terms(): row_total = jnp.sum(weights, axis=-1)  8.05 us
    all_to_all x1, starting transfers between devices, local(): lax.all_to_all(key_send, 'head', split_axis=1, concat_axis=0, tiled=True)  6.35 us
  transfers between devices with their start and end apart: 3, of which 2 were waited for; matrix products, arithmetic and copies ran while one was open for 5% of the time, Pallas kernels for 0%

commit v1 on v0

--- a/solution.py
+++ b/solution.py
@@ -82,7 +82,12 @@
         jnp.zeros(term_shape, jnp.float32),
         jnp.zeros(term_shape + (HEAD_SIZE,), jnp.float32),
     )
-    key_piece = lax.all_gather(key_block, "kv", axis=0, tiled=True)
+    ring = [key_block]
+    for hop in range(3):
+        ring.append(lax.ppermute(ring[-1], "kv", [(dev, (dev + 1) % 4) for dev in range(4)]))
+    key_piece = jnp.roll(
+        jnp.concatenate(ring[::-1], axis=0), (lax.axis_index("kv") + 1) * ring[0].shape[0], axis=0
+    )
     value_piece = lax.all_gather(value_block, "kv", axis=0, tiled=True)
     piece_rows = key_piece.shape[0]
     step_rows = math.gcd(piece_rows, 1024)

time: 177 us -> 170 us (0.960)
  blocking collectives: 94.4 us -> 83 us
  starting transfers between devices: 13.3 us -> 18.7 us
    all_gather x1 -> x0, blocking collectives: 9 us -> none  [local(): key_piece = lax.all_gather(key_block, 'kv', axis=0, tiled=True)]
    ppermute x0 -> x3, starting transfers between devices: none -> 5.41 us  [local(): lax.ppermute(ring[-1], 'kv', [(dev, (dev + 1) % 4) for dev in range(4)])]
    unnamed x7 -> x14, local copies, waits for them, and re-layouts: 3.49 us -> 3.62 us
  transfers between devices with their start and end apart: 3 -> 6, of which waited for: 2 -> 2; matrix products, arithmetic and copies ran while one was open for 5% -> 6% of each run, Pallas kernels for 0% -> 0%
where the time goes in v1:
time: 170 us
  blocking collectives  83 us (49%)
  local copies, waits for them, and re-layouts  28.6 us (17%)
  starting transfers between devices  18.7 us (11%)
  matrix products  18.3 us (11%)
  other arithmetic  11.8 us (7%)
  waiting for transfers between devices  8.04 us (5%)
    unnamed x1, blocking collectives  42.4 us
    all_to_all x1, blocking collectives, local(): lax.all_to_all(result, 'head', split_axis=0, concat_axis=1, tiled=True)  30 us
    dot_general x2, matrix products, block_terms(): jnp.einsum('kgrc,ckd->kgrd', weights.astype(jnp.bfloat16), value_heads, p...  12.5 us
    gather x2, local copies, waits for them, and re-layouts, one_step(): key_doc = jnp.take(doc_global, key_pos)  12.3 us
    all_gather x1, blocking collectives, local(): value_piece = lax.all_gather(value_block, 'kv', axis=0, tiled=True)  10.7 us
    reduce_sum x2, other arithmetic, block_terms(): row_total = jnp.sum(weights, axis=-1)  8.05 us
    all_to_all x1, starting transfers between devices, local(): lax.all_to_all(key_send, 'head', split_axis=1, concat_axis=0, tiled=True)  6.35 us
    dot_general x2, matrix products, block_terms(): jnp.einsum('rkgd,ckd->kgrc', query_group, key_heads, preferred_element_ty...  5.86 us
  transfers between devices with their start and end apart: 6, of which 2 were waited for; matrix products, arithmetic and copies ran while one was open for 6% of the time, Pallas kernels for 0%

profile of v1, /device:TPU:0, one launch (start us, length us, event | category | flops | bytes accessed | tf_op | source)
XLA Modules:
  0.0 169.8 jit_solution(11300037326310674453)
XLA Ops:
  0.0 0.0 copy-start
  0.0 0.9 copy-done
  0.9 0.7 copy_bitcast_fusion.2
  1.6 6.4 %all-to-all-start = ((bf16[64,8,128]{2,0,1:T(8,128)(2,1)}), bf16[64,8,128]{2,0,1:T(8,128)(2,1)S(1)}, u32[]{:S(2)}, u32[]{:S(2)}) async-start(bf16[64,8,128]{2,0,1:T(8,128)(2,1)} %copy_bitcast_fusion.2), calls=%async_computation | async-start | bytes 262144 | tf_op jit(solution)/shard_map/all_to_all | solution.py:66
  7.9 1.6 copy_bitcast_fusion.1
  9.5 5.2 %all-to-all-done = bf16[64,8,128]{2,0,1:T(8,128)(2,1)S(1)} async-done(((bf16[64,8,128]{2,0,1:T(8,128)(2,1)}), bf16[64,8,128]{2,0,1:T(8,128)(2,1)S(1)}, u32[]{:S(2)}, u32[]{:S(2)}) %all-to-all-start) | async-done | bytes 131104 | tf_op jit(solution)/shard_map/all_to_all | solution.py:66
  14.7 3.4 %all-to-all-start.2 = ((bf16[64,8,128]{2,0,1:T(8,128)(2,1)}), bf16[64,8,128]{2,0,1:T(8,128)(2,1)S(1)}, u32[]{:S(2)}, u32[]{:S(2)}) async-start(bf16[64,8,128]{2,0,1:T(8,128)(2,1)} %copy_bitcast_fusion.1), calls=%async_computation.2 | async-start | bytes 262144 | tf_op jit(solution)/shard_map/all_to_all | solution.py:67
  18.1 1.5 collective-permute-start
  19.6 2.3 %copy.30 = bf16[8,8,8,1024]{3,2,0,1:T(8,128)(2,1)} copy(bf16[8,8,8,1024]{3,2,1,0:T(8,128)(2,1)} %bitcast.124) | data formatting | bytes 2097152 | tf_op jit(solution)/shard_map/all_to_all | solution.py:65
  21.9 2.9 %all-to-all-done.2 = bf16[64,8,128]{2,0,1:T(8,128)(2,1)S(1)} async-done(((bf16[64,8,128]{2,0,1:T(8,128)(2,1)}), bf16[64,8,128]{2,0,1:T(8,128)(2,1)S(1)}, u32[]{:S(2)}, u32[]{:S(2)}) %all-to-all-start.2) | async-done | bytes 131104 | tf_op jit(solution)/shard_map/all_to_all | solution.py:67
  24.8 3.6 %all-to-all-start.1 = ((bf16[64,8,1024]{2,0,1:T(8,128)(2,1)}), bf16[64,8,1024]{2,0,1:T(8,128)(2,1)S(1)}, u32[]{:S(2)}, u32[]{:S(2)}) async-start(bf16[64,8,1024]{2,0,1:T(8,128)(2,1)} %bitcast.93), calls=%async_computation.1 | async-start | bytes 2097152 | tf_op jit(solution)/shard_map/all_to_all | solution.py:65
  28.3 0.0 collective-permute-done
  28.3 1.5 collective-permute-start.1
  29.9 1.3 dynamic-slice
  31.9 0.9 dynamic-update-slice
  32.8 42.4 %all-reduce = s32[2048]{0:T(1024)S(1)} all-reduce(s32[2048]{0:T(1024)S(1)} %dynamic-update-slice), channel_id=1, replica_groups=mesh['head'=8,'kv'=4] {'kv','head'}, use_global_device_ids=true, to_apply=%add | all-reduce | flops 2048 | bytes 16384
  75.1 3.1 %gather_fusion.1 = s32[512]{0:T(512)S(1)} fusion(s32[2048]{0:T(1024)S(1)} %all-reduce, s32[1024]{0:T(1024)S(1)} %pad_clamp_fusion), kind=kCustom, calls=%fused_computation.1 | custom fusion | bytes 6144 | tf_op jit(solution)/shard_map/jit(_take)/gather | solution.py:77
  78.3 0.0 collective-permute-done.1
  78.3 2.3 %collective-permute-start.2 = (bf16[512,128]{1,0:T(8,128)(2,1)S(1)}, bf16[512,128]{1,0:T(8,128)(2,1)S(1)}, u32[]{:S(2)}, u32[]{:S(2)}) collective-permute-start(bf16[512,128]{1,0:T(8,128)(2,1)S(1)} %collective-permute-done.1), channel_id=1, source_target_pairs={{0,1},{1,2},{2,3},{3,0},{4,5},{5,6},{6,7},{7,4},{8,9},{9,10},{10,1... | collective-permute-start | bytes 393224 | tf_op jit(solution)/shard_map/ppermute | solution.py:87
  80.6 10.7 %all_gather.7 = bf16[2048,128]{1,0:T(8,128)(2,1)S(1)} all-gather(bf16[512,128]{1,0:T(8,128)(2,1)S(1)} %bitcast.126), channel_id=1, replica_groups=mesh['head'=8,'kv'=4] {'kv'}, dimensions={0}, use_global_device_ids=true | all-gather | bytes 655360 | tf_op jit(solution)/shard_map/all_gather | solution.py:91
  91.3 0.0 collective-permute-done.2
  91.6 0.0 all-to-all-done.1
  91.6 0.3 copy.26
  91.9 0.1 copy.18
  92.0 43.6 %while.18 = (s32[]{:T(128)}, f32[1,8,512]{2,1,0:T(8,128)S(1)}, f32[1,8,512]{2,1,0:T(8,128)S(1)}, f32[1,8,512,128]{3,2,1,0:T(8,128)}, s32[2048]{0:T(1024)S(1)}, /...) while((s32[]{:T(128)}, f32[1,8,512]{2,1,0:T(8,128)S(1)}, ...), condition=%wide.region_3.4_spmd.clone, body=%wide.region_0.3_spmd.clone.sunk | while | flops 2205726208 | bytes 75335952 | solution.py:106
  92.3 6.2 %gather_fusion = s32[1024]{0:T(1024)S(1)} fusion(s32[2048]{0:T(1024)S(1)} %get-tuple-element.370, s32[1024]{0:T(1024)S(1)} %broadcast_clamp_fusion.2), kind=kCustom, calls=%fused_computation.clone.clone.1 | custom fusion | bytes 12288 | tf_op jit(solution)/shard_map/while/body/eval_jaxpr/jit(_take)/gather | solution.py:100
  98.5 0.8 compare_and_fusion.2
  99.3 2.9 %fusion.41 = (f32[8,512]{1,0:T(8,128)S(1)}, f32[1024,512,8]{1,0,2:T(8,128)S(1)}) fusion(pred[512,1024]{0,1:T(8,128)(4,1)S(1)} %compare_and_fusion.2, bf16[512,1,8,128]{3,0,2,1:T(8,128)(2,1)S(1)} %get-tuple-element.373, bf16[2048,128]{1,0:T(8,128)(2,1)S(1)} %get-tuple-element.372, s32[]{:T(128)S(6)} %select_n.160), kind=kOutput, calls=%fused_computation.5.clone.1 | convolution fusion | flops 1086320640 | bytes 18628612 | tf_op jit(solution)/shard_map/while/body/eval_jaxpr/rkgd,ckd->kgrc/dot_general | solution.py:27
  102.2 0.0 copy-start.1
  102.3 4.0 %fusion.43 = f32[8,512]{1,0:T(8,128)S(1)} fusion(f32[1024,512,8]{1,0,2:T(8,128)S(1)} %get-tuple-element.334, f32[8,512]{1,0:T(8,128)S(1)} %get-tuple-element.332, pred[512,1024]{0,1:T(8,128)(4,1)S(1)} %compare_and_fusion.2), kind=kLoop, calls=%fused_computation.7.clone.1 | loop fusion | flops 20967424 | bytes 17334272 | tf_op jit(solution)/shard_map/while/body/eval_jaxpr/reduce_sum | solution.py:34
  106.3 0.0 copy-done.1
  106.4 6.2 %bitcast_add_fusion.2 = f32[1,8,512,128]{3,2,1,0:T(8,128)S(1)} fusion(f32[1,8,512,128]{3,2,1,0:T(8,128)S(1)} %copy-done.1, f32[1024,512,8]{1,0,2:T(8,128)S(1)} %get-tuple-element.334, f32[8,512]{1,0:T(8,128)S(1)} %get-tuple-element.332, pred[512,1024]{0,1:T(8,128)(4,1)S(1)} %compare_and_fusion.2, f32[8,512]{1,0:T(8,128)S(1)} %get-tuple-element.336, ...), kind=kOutput, calls=%fused_computation.11.clone.1 | convolution fusion | flops 1096810496 | bytes 21807108 | tf_op jit(solution)/shard_map/while/body/eval_jaxpr/kgrc,ckd->kgrd/dot_general | solution.py:35
  112.6 0.0 copy-start.2
  112.6 1.3 copy-done.2
  114.0 6.2 %gather_fusion = s32[1024]{0:T(1024)S(1)} fusion(s32[2048]{0:T(1024)S(1)} %get-tuple-element.370, s32[1024]{0:T(1024)S(1)} %broadcast_clamp_fusion.2), kind=kCustom, calls=%fused_computation.clone.clone.1 | custom fusion | bytes 12288 | tf_op jit(solution)/shard_map/while/body/eval_jaxpr/jit(_take)/gather | solution.py:100
  120.2 0.8 compare_and_fusion.2
  121.0 2.9 %fusion.41 = (f32[8,512]{1,0:T(8,128)S(1)}, f32[1024,512,8]{1,0,2:T(8,128)S(1)}) fusion(pred[512,1024]{0,1:T(8,128)(4,1)S(1)} %compare_and_fusion.2, bf16[512,1,8,128]{3,0,2,1:T(8,128)(2,1)S(1)} %get-tuple-element.373, bf16[2048,128]{1,0:T(8,128)(2,1)S(1)} %get-tuple-element.372, s32[]{:T(128)S(6)} %select_n.160), kind=kOutput, calls=%fused_computation.5.clone.1 | convolution fusion | flops 1086320640 | bytes 18628612 | tf_op jit(solution)/shard_map/while/body/eval_jaxpr/rkgd,ckd->kgrc/dot_general | solution.py:27
  124.0 0.0 copy-start.1
  124.0 4.0 %fusion.43 = f32[8,512]{1,0:T(8,128)S(1)} fusion(f32[1024,512,8]{1,0,2:T(8,128)S(1)} %get-tuple-element.334, f32[8,512]{1,0:T(8,128)S(1)} %get-tuple-element.332, pred[512,1024]{0,1:T(8,128)(4,1)S(1)} %compare_and_fusion.2), kind=kLoop, calls=%fused_computation.7.clone.1 | loop fusion | flops 20967424 | bytes 17334272 | tf_op jit(solution)/shard_map/while/body/eval_jaxpr/reduce_sum | solution.py:34
  128.1 0.0 copy-done.1
  128.1 6.2 %bitcast_add_fusion.2 = f32[1,8,512,128]{3,2,1,0:T(8,128)S(1)} fusion(f32[1,8,512,128]{3,2,1,0:T(8,128)S(1)} %copy-done.1, f32[1024,512,8]{1,0,2:T(8,128)S(1)} %get-tuple-element.334, f32[8,512]{1,0:T(8,128)S(1)} %get-tuple-element.332, pred[512,1024]{0,1:T(8,128)(4,1)S(1)} %compare_and_fusion.2, f32[8,512]{1,0:T(8,128)S(1)} %get-tuple-element.336, ...), kind=kOutput, calls=%fused_computation.11.clone.1 | convolution fusion | flops 1096810496 | bytes 21807108 | tf_op jit(solution)/shard_map/while/body/eval_jaxpr/kgrc,ckd->kgrd/dot_general | solution.py:35
  134.3 0.0 copy-start.2
  134.3 1.3 copy-done.2
  135.7 2.0 %fusion.26 = bf16[512,1,8,128]{3,0,2,1:T(8,128)(2,1)S(1)} fusion(f32[1,8,512,128]{3,2,1,0:T(8,128)} %get-tuple-element.175, f32[8,512]{1,0:T(8,128)S(1)} %bitcast.125), kind=kLoop, calls=%fused_computation.42 | loop fusion | flops 1048576 | bytes 3162112 | tf_op jit(solution)/shard_map/convert_element_type | solution.py:110
  137.6 0.7 copy.19
  138.3 0.5 convert_element_type.19
  138.8 30.0 %all_to_all.70 = bf16[8,64,1024]{2,1,0:T(8,128)(2,1)S(1)} all-to-all(bf16[8,64,1024]{2,1,0:T(8,128)(2,1)S(1)} %convert_element_type.19), channel_id=1, replica_groups=mesh['head'=8,'kv'=4] {'head'}, dimensions={0} | all-to-all | bytes 2097152 | tf_op jit(solution)/shard_map/all_to_all | solution.py:111
  168.8 1.1 copy.25
  (30 shorter events, 0.3 us)
Async XLA Ops:
  0.0 0.9 copy-start
  1.6 13.1 %all-to-all-start = ((bf16[64,8,128]{2,0,1:T(8,128)(2,1)}), bf16[64,8,128]{2,0,1:T(8,128)(2,1)S(1)}, u32[]{:S(2)}, u32[]{:S(2)}) async-start(bf16[64,8,128]{2,0,1:T(8,128)(2,1)} %copy_bitcast_fusion.2), calls=%async_computation | async-start | bytes 262144 | tf_op jit(solution)/shard_map/all_to_all | solution.py:66
  14.7 10.1 %all-to-all-start.2 = ((bf16[64,8,128]{2,0,1:T(8,128)(2,1)}), bf16[64,8,128]{2,0,1:T(8,128)(2,1)S(1)}, u32[]{:S(2)}, u32[]{:S(2)}) async-start(bf16[64,8,128]{2,0,1:T(8,128)(2,1)} %copy_bitcast_fusion.1), calls=%async_computation.2 | async-start | bytes 262144 | tf_op jit(solution)/shard_map/all_to_all | solution.py:67
  18.1 10.3 %collective-permute-start = (bf16[512,128]{1,0:T(8,128)(2,1)S(1)}, bf16[512,128]{1,0:T(8,128)(2,1)S(1)}, u32[]{:S(2)}, u32[]{:S(2)}) collective-permute-start(bf16[512,128]{1,0:T(8,128)(2,1)S(1)} %bitcast.121), channel_id=1, source_target_pairs={{0,1},{1,2},{2,3},{3,0},{4,5},{5,6},{6,7},{7,4},{8,9},{9,10},{10,1... | collective-permute-start | bytes 393224 | tf_op jit(solution)/shard_map/ppermute | solution.py:87
  24.8 66.9 %all-to-all-start.1 = ((bf16[64,8,1024]{2,0,1:T(8,128)(2,1)}), bf16[64,8,1024]{2,0,1:T(8,128)(2,1)S(1)}, u32[]{:S(2)}, u32[]{:S(2)}) async-start(bf16[64,8,1024]{2,0,1:T(8,128)(2,1)} %bitcast.93), calls=%async_computation.1 | async-start | bytes 2097152 | tf_op jit(solution)/shard_map/all_to_all | solution.py:65
  28.3 49.9 %collective-permute-start.1 = (bf16[512,128]{1,0:T(8,128)(2,1)S(1)}, bf16[512,128]{1,0:T(8,128)(2,1)S(1)}, u32[]{:S(2)}, u32[]{:S(2)}) collective-permute-start(bf16[512,128]{1,0:T(8,128)(2,1)S(1)} %collective-permute-done), channel_id=1, source_target_pairs={{0,1},{1,2},{2,3},{3,0},{4,5},{5,6},{6,7},{7,4},{8,9},{9,10},{10,1... | collective-permute-start | bytes 393224 | tf_op jit(solution)/shard_map/ppermute | solution.py:87
  78.3 13.1 %collective-permute-start.2 = (bf16[512,128]{1,0:T(8,128)(2,1)S(1)}, bf16[512,128]{1,0:T(8,128)(2,1)S(1)}, u32[]{:S(2)}, u32[]{:S(2)}) collective-permute-start(bf16[512,128]{1,0:T(8,128)(2,1)S(1)} %collective-permute-done.1), channel_id=1, source_target_pairs={{0,1},{1,2},{2,3},{3,0},{4,5},{5,6},{6,7},{7,4},{8,9},{9,10},{10,1... | collective-permute-start | bytes 393224 | tf_op jit(solution)/shard_map/ppermute | solution.py:87
  102.2 4.1 %copy-start.1 = (f32[1,8,512,128]{3,2,1,0:T(8,128)S(1)}, f32[1,8,512,128]{3,2,1,0:T(8,128)}, u32[]{:S(2)}) copy-start(f32[1,8,512,128]{3,2,1,0:T(8,128)} %get-tuple-element.355) | copy-start | bytes 6291460 | tf_op jit(solution)/shard_map/while
  112.6 1.3 copy-start.2
  124.0 4.1 %copy-start.1 = (f32[1,8,512,128]{3,2,1,0:T(8,128)S(1)}, f32[1,8,512,128]{3,2,1,0:T(8,128)}, u32[]{:S(2)}) copy-start(f32[1,8,512,128]{3,2,1,0:T(8,128)} %get-tuple-element.355) | copy-start | bytes 6291460 | tf_op jit(solution)/shard_map/while
  134.3 1.3 copy-start.2
